TPU v7x, 32 devices: a whole 2x2x4 slice. The times are simulated.
32 devices in a mesh: row: 2 (over x), col: 4 (over z), depth: 4 (over y, core).
Axes of the slice: x: 2, y: 2, z: 4, core: 2. Of those that a mesh axis runs over, the one named last changes fastest.
Arguments:
- pair: bfloat16 [768, 768, 128], P('row', 'col'), may hold values from -6 to 6
- ln_gain: float32 [128], replicated, may hold values from 0.1 to 1.9
- ln_shift: float32 [128], replicated, may hold values from -3 to 3
- proj_weight: bfloat16 [128, 512], replicated, may hold values from -0.5 to 0.5
- proj_bias: float32 [512], replicated, may hold values from -3 to 3
- gate_weight: bfloat16 [128, 128], replicated, may hold values from -0.5 to 0.5
- gate_bias: float32 [128], replicated, may hold values from -3 to 3
- out_gain: float32 [128], replicated, may hold values from 0.1 to 1.9
- out_shift: float32 [128], replicated, may hold values from -3 to 3
- out_weight: bfloat16 [128, 128], replicated, may hold values from -0.5 to 0.5
- out_bias: float32 [128], replicated, may hold values from -3 to 3
Outputs:
- update: bfloat16 [768, 768, 128], P('row', 'col')
All inputs are finite; a program needn't handle non-finite values.
Results may differ from a plain program's by a relative error of at most 0.0051.
Values may be sent and summed in bfloat16 or wider, within the bound.
No kernel may reach another device: no remote copies, remote signals or barrier semaphores. Data moves between devices by JAX's collectives and lax.ppermute only.
A program may use at most 256 MiB of HBM per device.

v0:
```python
import jax
import jax.numpy as jnp
from jax import lax
from jax.sharding import PartitionSpec as P


def layer_norm(values, gain, shift):
    centre = jnp.mean(values, axis=-1, keepdims=True)
    centred = values - centre
    spread = jnp.mean(centred * centred, axis=-1, keepdims=True)
    return centred * lax.rsqrt(spread + 1e-05) * gain + shift


def project(piece, ln_gain, ln_shift, proj_weight, proj_bias, gate_weight, gate_bias):
    hidden = proj_weight.shape[1] // 4
    channels = piece.shape[2]
    normed = layer_norm(piece.astype(jnp.float32), ln_gain, ln_shift).astype(jnp.bfloat16)
    flat = normed.reshape(-1, channels)
    mixed = jnp.dot(flat, proj_weight, preferred_element_type=jnp.float32) + proj_bias
    left = (jax.nn.sigmoid(mixed[:, :hidden]) * mixed[:, hidden : 2 * hidden]).astype(jnp.bfloat16)
    right = (jax.nn.sigmoid(mixed[:, 2 * hidden : 3 * hidden]) * mixed[:, 3 * hidden :]).astype(
        jnp.bfloat16
    )
    gate = jax.nn.sigmoid(
        jnp.dot(flat, gate_weight, preferred_element_type=jnp.float32) + gate_bias
    )
    shape = (piece.shape[0], piece.shape[1])
    return (
        left.reshape(shape + (hidden,)),
        right.reshape(shape + (hidden,)),
        gate.reshape(shape + (channels,)),
    )


def finish(triangle, gate, out_gain, out_shift, out_weight, out_bias):
    hidden = triangle.shape[2]
    tri_normed = layer_norm(triangle, out_gain, out_shift).astype(jnp.bfloat16)
    projected = (
        jnp.dot(tri_normed.reshape(-1, hidden), out_weight, preferred_element_type=jnp.float32)
        + out_bias
    )
    return (gate * projected.reshape(gate.shape)).astype(jnp.bfloat16)


def per_device(
    pair,
    ln_gain,
    ln_shift,
    proj_weight,
    proj_bias,
    gate_weight,
    gate_bias,
    out_gain,
    out_shift,
    out_weight,
    out_bias,
):
    depth_count = lax.axis_size("depth")
    depth_id = lax.axis_index("depth")
    cols_here = pair.shape[1]
    quarter = cols_here // depth_count
    piece = lax.dynamic_slice_in_dim(pair, depth_id * quarter, quarter, 1)
    left, right, gate = project(
        piece, ln_gain, ln_shift, proj_weight, proj_bias, gate_weight, gate_bias
    )
    left_all = lax.all_gather(left, ("col", "depth"), axis=1, tiled=True)
    right_column = lax.all_gather(right, "row", axis=0, tiled=True)
    needed = lax.all_to_all(right_column, ("col", "depth"), split_axis=0, concat_axis=1, tiled=True)
    triangle = jnp.einsum("ikc,jkc->ijc", left_all, needed, preferred_element_type=jnp.float32)
    finished = finish(triangle, gate, out_gain, out_shift, out_weight, out_bias)
    return lax.all_gather(finished, "depth", axis=1, tiled=True)


def solution(mesh):
    placed = (P("row", "col", None), P(), P(), P(), P(), P(), P(), P(), P(), P(), P())
    return jax.shard_map(
        per_device, mesh=mesh, in_specs=placed, out_specs=P("row", "col", None), check_vma=False
    )
```

profile of v0, /device:TPU:0, one launch (start us, length us, event | category | flops | bytes accessed | tf_op | source)
XLA Modules:
  0.0 949.2 jit_solution(18416673488483238151)
XLA Ops:
  6.5 0.0 copy-start
  6.5 0.0 all-gather.4.cloned.1.call-start
  6.6 0.0 copy-start.5
  6.6 4.9 convert_reduce_fusion
  11.5 0.1 copy.41
  11.6 0.1 copy.42
  11.8 7.2 fusion.8
  18.9 0.1 copy.43
  19.1 0.1 copy.44
  19.2 0.0 copy-done.10
  19.2 0.0 copy-done.9
  19.2 7.0 fusion.11
  26.3 0.0 copy-start.3
  26.3 0.0 copy-done
  26.3 0.0 copy-done.5
  26.3 14.7 %convolution_add_fusion = f32[18432,512]{1,0:T(8,128)} fusion(bf16[18432,128]{1,0:T(8,128)(2,1)S(1)} %bitcast.27, bf16[128,512]{1,0:T(8,128)(2,1)S(1)} %copy-done, f32[512]{0:T(512)S(1)} %copy-done.5), kind=kOutput, calls=%fused_computation | convolution fusion | flops 2425356288 | bytes 42600448 | tf_op jit(solution)/shard_map/dot_general | solution.py:19
  41.0 0.0 copy-done.3
  41.0 17.7 %fusion.12 = (bf16[18432,128]{1,0:T(8,128)(2,1)}, bf16[18432,128]{1,0:T(8,128)(2,1)}) fusion(f32[18432,512]{1,0:T(8,128)} %convolution_add_fusion), kind=kLoop, calls=%fused_computation.18 | loop fusion | flops 23592960 | bytes 47185920 | tf_op jit(solution)/shard_map/convert_element_type | solution.py:20
  58.8 0.0 all-gather.4.cloned.1.call-update
  58.8 0.0 all-gather.6.cloned.1.call-start
  58.9 7.6 copy.46
  66.4 0.0 all-gather.6.cloned.1.call-update
  66.5 0.0 copy-start.11
  66.5 0.0 copy-start.12
  66.5 113.2 %all-gather.4.cloned.1.call-done = bf16[768,48,128]{2,1,0:T(8,128)(2,1)} async-done(((bf16[384,48,128]{2,1,0:T(8,128)(2,1)}), bf16[768,48,128]{2,1,0:T(8,128)(2,1)}) %all-gather.4.cloned.1.call-update) | async-done | bytes 9437200 | tf_op jit(solution)/shard_map/all_gather | solution.py:67
  179.7 5.7 all-to-all-start
  185.3 0.2 all-gather.8.cloned.1.call-start
  185.6 0.0 copy-done.11
  185.6 0.0 copy-done.12
  185.6 8.9 fusion.5
  194.4 299.5 %all-to-all-done = bf16[768,48,128]{2,1,0:T(8,128)(2,1)} async-done(((bf16[768,48,128]{2,1,0:T(8,128)(2,1)}), bf16[768,48,128]{2,1,0:T(8,128)(2,1)}, u32[]{:S(2)}, u32[]{:S(2)}) %all-to-all-start) | async-done | bytes 9437216 | tf_op jit(solution)/shard_map/all_to_all | solution.py:68
  493.9 10.1 %copy.45 = bf16[48,16,48,128]{3,2,1,0:T(8,128)(2,1)} copy(bf16[48,16,48,128]{3,2,0,1:T(8,128)(2,1)} %bitcast.3) | data formatting | bytes 18874368 | tf_op jit(solution)/shard_map/all_to_all | solution.py:68
  504.0 13.3 %copy.47 = bf16[48,768,128]{1,0,2:T(8,128)(2,1)} copy(bf16[48,768,128]{2,1,0:T(8,128)(2,1)} %bitcast.24) | data formatting | bytes 18874368 | tf_op jit(solution)/shard_map/all_to_all | solution.py:68
  517.2 195.3 %all-gather.6.cloned.1.call-done = bf16[384,768,128]{0,1,2:T(8,128)(2,1)} async-done(((bf16[384,48,128]{0,1,2:T(8,128)(2,1)}), bf16[384,768,128]{0,1,2:T(8,128)(2,1)}) %all-gather.6.cloned.1.call-update) | async-done | bytes 75497488 | tf_op jit(solution)/shard_map/all_gather | solution.py:66
  712.6 32.4 %bitcast_reduce_fusion = (f32[384,48]{0,1:T(8,128)S(1)}, f32[128,48,384]{2,1,0:T(8,128)}) fusion(bf16[48,768,128]{1,0,2:T(8,128)(2,1)} %copy.47, bf16[384,768,128]{0,1,2:T(8,128)(2,1)} %all-gather.6.cloned.1.call-done), kind=kOutput, calls=%fused_computation.30 | convolution fusion | flops 3626219520 | bytes 94445568 | tf_op jit(solution)/shard_map/ikc,jkc->ijc/dot_general | solution.py:69
  745.0 4.8 multiply_reduce_fusion
  749.9 1.5 copy-done.2
  751.4 0.0 copy-done.7
  751.4 0.0 copy-done.8
  751.4 3.8 add_convert_fusion
  755.2 7.5 copy.48
  762.7 0.0 copy-done.4
  762.7 0.0 copy-done.6
  762.7 8.7 fusion.4
  771.4 0.0 all-gather.8.cloned.1.call-update
  771.5 153.4 %all-gather.8.cloned.1.call-done = bf16[384,192,128]{2,1,0:T(8,128)(2,1)} async-done(((bf16[384,48,128]{2,1,0:T(8,128)(2,1)}), bf16[384,192,128]{2,1,0:T(8,128)(2,1)}) %all-gather.8.cloned.1.call-update) | async-done | bytes 18874384 | tf_op jit(solution)/shard_map/all_gather | solution.py:71
  924.9 17.8 %copy.50 = bf16[384,192,128]{2,1,0:T(8,128)(2,1)} copy(bf16[384,192,128]{2,1,0:T(8,128)(2,1)} %all-gather.8.cloned.1.call-done) | data formatting | bytes 37748736
  942.6 0.0 copy-done.1
  (12 shorter events, 0.1 us)
Async XLA Ops:
  6.5 19.8 %copy-start = (bf16[128,512]{1,0:T(8,128)(2,1)S(1)}, bf16[128,512]{1,0:T(8,128)(2,1)}, u32[]{:S(2)}) copy-start(bf16[128,512]{1,0:T(8,128)(2,1)} %param.14) | copy-start | bytes 393220
  6.5 12.7 %copy-start.10 = (f32[128]{0:T(128)S(1)}, f32[128]{0:T(128)}, u32[]{:S(2)}) copy-start(f32[128]{0:T(128)} %param.12) | copy-start | bytes 1540
  6.5 12.7 %copy-start.9 = (f32[128]{0:T(128)S(1)}, f32[128]{0:T(128)}, u32[]{:S(2)}) copy-start(f32[128]{0:T(128)} %param.13) | copy-start | bytes 1540
  6.5 173.1 %all-gather.4.cloned.1.call-start = ((), (), s32[]{:S(2)}) async-start(), calls=%async_computation.1 | async-start | bytes 14155776 | tf_op jit(solution)/shard_map/all_gather | solution.py:67
  6.6 19.7 %copy-start.5 = (f32[512]{0:T(512)S(1)}, f32[512]{0:T(512)}, u32[]{:S(2)}) copy-start(f32[512]{0:T(512)} %param.15) | copy-start | bytes 6148
  26.3 14.8 %copy-start.3 = (bf16[384,48,128]{2,1,0:T(8,128)(2,1)}, bf16[384,48,128]{2,1,0:T(8,128)(2,1)S(1)}, u32[]{:S(2)}) copy-start(bf16[384,48,128]{2,1,0:T(8,128)(2,1)S(1)} %fusion.11) | copy-start | bytes 14155780
  58.8 653.8 %all-gather.6.cloned.1.call-start = ((), (), s32[]{:S(2)}) async-start(), calls=%async_computation.2 | async-start | bytes 80216064 | tf_op jit(solution)/shard_map/all_gather | solution.py:66
  66.5 119.1 %copy-start.11 = (bf16[128,128]{1,0:T(8,128)(2,1)S(1)}, bf16[128,128]{1,0:T(8,128)(2,1)}, u32[]{:S(2)}) copy-start(bf16[128,128]{1,0:T(8,128)(2,1)} %param.16) | copy-start | bytes 98308
  66.5 119.1 %copy-start.12 = (f32[128]{0:T(128)S(1)}, f32[128]{0:T(128)}, u32[]{:S(2)}) copy-start(f32[128]{0:T(128)} %param.17) | copy-start | bytes 1540
  179.7 314.3 %all-to-all-start = ((bf16[768,48,128]{2,1,0:T(8,128)(2,1)}), bf16[768,48,128]{2,1,0:T(8,128)(2,1)}, u32[]{:S(2)}, u32[]{:S(2)}) async-start(bf16[768,48,128]{2,1,0:T(8,128)(2,1)} %all-gather.4.cloned.1.call-done), calls=%async_computation | async-start | bytes 18874368 | tf_op jit(solution)/shard_map/all_to_all | solution.py:68
  185.3 739.5 %all-gather.8.cloned.1.call-start = ((), (), s32[]{:S(2)}) async-start(), calls=%async_computation.3 | async-start | bytes 23592960 | tf_op jit(solution)/shard_map/all_gather | solution.py:71
  745.0 6.4 copy-start.2
  745.0 6.4 copy-start.7
  745.0 6.4 copy-start.8
  751.4 11.3 %copy-start.4 = (bf16[128,128]{1,0:T(8,128)(2,1)S(1)}, bf16[128,128]{1,0:T(8,128)(2,1)}, u32[]{:S(2)}) copy-start(bf16[128,128]{1,0:T(8,128)(2,1)} %param.20) | copy-start | bytes 98308
  751.4 11.3 %copy-start.6 = (f32[128]{0:T(128)S(1)}, f32[128]{0:T(128)}, u32[]{:S(2)}) copy-start(f32[128]{0:T(128)} %param.21) | copy-start | bytes 1540
  924.9 17.8 %copy-start.1 = (bf16[128,512]{1,0:T(8,128)(2,1)S(1)}, bf16[128,512]{1,0:T(8,128)(2,1)}, u32[]{:S(2)}) copy-start(bf16[128,512]{1,0:T(8,128)(2,1)} %param.14) | copy-start | bytes 393220
Sparse Core Ops, SparseCore 0:
  58.9 120.6 all-gather.3
  181.2 531.3 all-gather.5
  771.6 153.2 all-gather.7
where the time goes:
time: 950 us; the launch traced here: 949 us
  waiting for transfers between devices  761 us (80%)
  matrix products  64.7 us (7%)
  local copies, waits for them, and re-layouts  58.2 us (6%)
  other arithmetic  45.6 us (5%)
  between operations  13.3 us (1%)
    all_to_all x1, waiting for transfers between devices, per_device(): lax.all_to_all(right_column, ('col', 'depth'), split_axis=0, concat_axis=...  299 us
    all_gather x1, waiting for transfers between devices, per_device(): left_all = lax.all_gather(left, ('col', 'depth'), axis=1, tiled=True)  195 us
    all_gather x1, waiting for transfers between devices, per_device(): return lax.all_gather(finished, 'depth', axis=1, tiled=True)  153 us
    all_gather x1, waiting for transfers between devices, per_device(): right_column = lax.all_gather(right, 'row', axis=0, tiled=True)  113 us
    dot_general x1, matrix products, per_device(): jnp.einsum('ikc,jkc->ijc', left_all, needed, preferred_element_type=jnp.f...  32.4 us
    all_to_all x2, local copies, waits for them, and re-layouts, per_device(): lax.all_to_all(right_column, ('col', 'depth'), split_axis=0, concat_axis=...  23.3 us
    unnamed x27, local copies, waits for them, and re-layouts  19.3 us
  transfers between devices with their start and end apart: 4, of which 4 were waited for; matrix products, arithmetic and copies ran while one was open for 4% of the time, Pallas kernels for 0%

commit v1 on v0

--- a/solution.py
+++ b/solution.py
@@ -63,10 +63,43 @@
     left, right, gate = project(
         piece, ln_gain, ln_shift, proj_weight, proj_bias, gate_weight, gate_bias
     )
-    left_all = lax.all_gather(left, ("col", "depth"), axis=1, tiled=True)
     right_column = lax.all_gather(right, "row", axis=0, tiled=True)
     needed = lax.all_to_all(right_column, ("col", "depth"), split_axis=0, concat_axis=1, tiled=True)
-    triangle = jnp.einsum("ikc,jkc->ijc", left_all, needed, preferred_element_type=jnp.float32)
+    size, position, rows = (
+        lax.axis_size(("col", "depth")),
+        lax.axis_index(("col", "depth")),
+        left.shape[1],
+    )
+    forward = [(i, (i + 1) % size) for i in range(size)]
+    behind = [(i, (i - 1) % size) for i in range(size)]
+    half = size // 2
+    from_left = from_right = left
+    triangle = jnp.einsum(
+        "ikc,jkc->ijc",
+        left,
+        lax.dynamic_slice_in_dim(needed, position * rows, left.shape[1], axis=1),
+        preferred_element_type=jnp.float32,
+    )
+    for step in range(1, half + 1):
+        from_left = lax.ppermute(from_left, ("col", "depth"), forward)
+        if step < size - half:
+            from_right = lax.ppermute(from_right, ("col", "depth"), behind)
+            triangle = triangle + jnp.einsum(
+                "ikc,jkc->ijc",
+                from_right,
+                lax.dynamic_slice_in_dim(
+                    needed, (position + step) % size * rows, from_right.shape[1], axis=1
+                ),
+                preferred_element_type=jnp.float32,
+            )
+        triangle = triangle + jnp.einsum(
+            "ikc,jkc->ijc",
+            from_left,
+            lax.dynamic_slice_in_dim(
+                needed, (position - step) % size * rows, from_left.shape[1], axis=1
+            ),
+            preferred_element_type=jnp.float32,
+        )
     finished = finish(triangle, gate, out_gain, out_shift, out_weight, out_bias)
     return lax.all_gather(finished, "depth", axis=1, tiled=True)
 

time: 950 us -> 1240 us (1.31)
  starting transfers between devices: 5.93 us -> 554 us
  waiting for transfers between devices: 761 us -> 337 us
  matrix products: 64.7 us -> 190 us
  local copies, waits for them, and re-layouts: 58.2 us -> 93.4 us
    ppermute x0 -> x15, starting transfers between devices: none -> 548 us  [the longest x8 531 us: per_device(): from_left = lax.ppermute(from_left, ('col', 'depth'), forward)]
    all_to_all x1, waiting for transfers between devices: 299 us -> 0.01 us  [per_device(): lax.all_to_all(right_column, ('col', 'depth'), split_axis=0, concat_axis=...]
    all_gather x1 -> x0, waiting for transfers between devices: 195 us -> none  [per_device(): left_all = lax.all_gather(left, ('col', 'depth'), axis=1, tiled=True)]
    ppermute x0 -> x15, waiting for transfers between devices: none -> 170 us  [the longest x7 92.6 us: per_device(): from_right = lax.ppermute(from_right, ('col', 'depth'), behind)]
    dot_general x1 -> x16, matrix products: 32.4 us -> 158 us  [the longest x8 101 us: per_device(): jnp.einsum('ikc,jkc->ijc', from_left, lax.dynamic_slice_in_dim(needed, (p...]
    all_gather x1, waiting for transfers between devices: 113 us -> 0.01 us  [per_device(): right_column = lax.all_gather(right, 'row', axis=0, tiled=True)]
    unnamed x27 -> x87, local copies, waits for them, and re-layouts: 19.3 us -> 60.4 us
    all_gather x1, waiting for transfers between devices: 153 us -> 167 us  [per_device(): return lax.all_gather(finished, 'depth', axis=1, tiled=True)]
  transfers between devices with their start and end apart: 4 -> 18, of which waited for: 4 -> 6; matrix products, arithmetic and copies ran while one was open for 4% -> 14% of each run, Pallas kernels for 0% -> 0%
where the time goes in v1:
time: 1240 us; the launch traced here: 1230 us
  starting transfers between devices  554 us (45%)
  waiting for transfers between devices  337 us (27%)
  matrix products  190 us (15%)
  local copies, waits for them, and re-layouts  93.4 us (8%)
  other arithmetic  45.5 us (4%)
  between operations  13.9 us (1%)
    ppermute x8, starting transfers between devices, per_device(): from_left = lax.ppermute(from_left, ('col', 'depth'), forward)  531 us
    all_gather x1, waiting for transfers between devices, per_device(): return lax.all_gather(finished, 'depth', axis=1, tiled=True)  167 us
    dot_general x8, matrix products, per_device(): jnp.einsum('ikc,jkc->ijc', from_left, lax.dynamic_slice_in_dim(needed, (p...  101 us
    ppermute x7, waiting for transfers between devices, per_device(): from_right = lax.ppermute(from_right, ('col', 'depth'), behind)  92.6 us
    ppermute x8, waiting for transfers between devices, per_device(): from_left = lax.ppermute(from_left, ('col', 'depth'), forward)  77.5 us
    unnamed x87, local copies, waits for them, and re-layouts  60.4 us
    dot_general x7, matrix products, per_device(): jnp.einsum('ikc,jkc->ijc', from_right, lax.dynamic_slice_in_dim(needed, (...  47.8 us
  transfers between devices with their start and end apart: 18, of which 6 were waited for; matrix products, arithmetic and copies ran while one was open for 14% of the time, Pallas kernels for 0%

profile of v1, /device:TPU:0, one launch (start us, length us, event | category | flops | bytes accessed | tf_op | source)
XLA Modules:
  0.0 1233.7 jit_solution(14483596100839880992)
XLA Ops:
  6.5 4.9 convert_reduce_fusion
  11.7 7.2 fusion.8
  19.2 7.0 fusion.11
  26.3 14.8 %convolution_add_fusion = f32[18432,512]{1,0:T(8,128)} fusion(bf16[18432,128]{1,0:T(8,128)(2,1)S(1)} %bitcast.57, bf16[128,512]{1,0:T(8,128)(2,1)S(1)} %copy-done, f32[512]{0:T(512)S(1)} %copy-done.21), kind=kOutput, calls=%fused_computation | convolution fusion | flops 2425356288 | bytes 42600448 | tf_op jit(solution)/shard_map/dot_general | solution.py:19
  41.0 17.7 %fusion.12 = (bf16[18432,128]{1,0:T(8,128)(2,1)}, bf16[18432,128]{1,0:T(8,128)(2,1)}) fusion(f32[18432,512]{1,0:T(8,128)} %convolution_add_fusion), kind=kLoop, calls=%fused_computation.18 | loop fusion | flops 23592960 | bytes 47185920 | tf_op jit(solution)/shard_map/convert_element_type | solution.py:20
  58.8 7.6 copy.117
  66.9 5.0 collective-permute-start
  71.9 52.1 %collective-permute-done.1 = bf16[384,48,128]{0,1,2:T(8,128)(2,1)} collective-permute-done((bf16[384,48,128]{0,1,2:T(8,128)(2,1)}, bf16[384,48,128]{0,1,2:T(8,128)(2,1)}, u32[]{:S(2)}, u32[]{:S(2)}) %collective-permute-start.1) | collective-permute-done | bytes 4718624 | tf_op jit(solution)/shard_map/ppermute | solution.py:84
  124.1 47.4 %collective-permute-start.3 = (bf16[384,48,128]{0,1,2:T(8,128)(2,1)}, bf16[384,48,128]{0,1,2:T(8,128)(2,1)}, u32[]{:S(2)}, u32[]{:S(2)}) collective-permute-start(bf16[384,48,128]{0,1,2:T(8,128)(2,1)} %collective-permute-done.1), channel_id=1, source_target_pairs={{0,1},{1,2},{2,3},{3,4},{4,5},{5,6},{6,7},{7,8},{8,9},{9,10},{10,1... | collective-permute-start | bytes 14155784 | tf_op jit(solution)/shard_map/ppermute | solution.py:84
  171.4 9.3 collective-permute-done.3
  180.7 94.4 %collective-permute-start.5 = (bf16[384,48,128]{0,1,2:T(8,128)(2,1)}, bf16[384,48,128]{0,1,2:T(8,128)(2,1)}, u32[]{:S(2)}, u32[]{:S(2)}) collective-permute-start(bf16[384,48,128]{0,1,2:T(8,128)(2,1)} %collective-permute-done.3), channel_id=1, source_target_pairs={{0,1},{1,2},{2,3},{3,4},{4,5},{5,6},{6,7},{7,8},{8,9},{9,10},{10,1... | collective-permute-start | bytes 14155784 | tf_op jit(solution)/shard_map/ppermute | solution.py:84
  275.1 6.1 all-to-all-start
  281.3 4.4 collective-permute-start.4
  285.6 106.8 %collective-permute-start.7 = (bf16[384,48,128]{0,1,2:T(8,128)(2,1)}, bf16[384,48,128]{0,1,2:T(8,128)(2,1)S(1)}, u32[]{:S(2)}, u32[]{:S(2)}) collective-permute-start(bf16[384,48,128]{0,1,2:T(8,128)(2,1)} %collective-permute-done.5), channel_id=1, source_target_pairs={{0,1},{1,2},{2,3},{3,4},{4,5},{5,6},{6,7},{7,8},{8,9},{9,10},{10,1... | collective-permute-start | bytes 14155784 | tf_op jit(solution)/shard_map/ppermute | solution.py:84
  392.4 92.6 %collective-permute-done.4 = bf16[384,48,128]{0,1,2:T(8,128)(2,1)S(1)} collective-permute-done((bf16[384,48,128]{0,1,2:T(8,128)(2,1)}, bf16[384,48,128]{0,1,2:T(8,128)(2,1)S(1)}, u32[]{:S(2)}, u32[]{:S(2)}) %collective-permute-start.4) | collective-permute-done | bytes 4718624 | tf_op jit(solution)/shard_map/ppermute | solution.py:86
  487.2 4.7 collective-permute-start.6
  491.9 140.5 %collective-permute-start.9 = (bf16[384,48,128]{0,1,2:T(8,128)(2,1)S(1)}, bf16[384,48,128]{0,1,2:T(8,128)(2,1)}, u32[]{:S(2)}, u32[]{:S(2)}) collective-permute-start(bf16[384,48,128]{0,1,2:T(8,128)(2,1)S(1)} %collective-permute-done.7), channel_id=1, source_target_pairs={{0,1},{1,2},{2,3},{3,4},{4,5},{5,6},{6,7},{7,8},{8,9},{9,10},{10,1... | collective-permute-start | bytes 14155784 | tf_op jit(solution)/shard_map/ppermute | solution.py:84
  632.4 7.6 collective-permute-done.9
  640.0 45.8 %collective-permute-start.11 = (bf16[384,48,128]{0,1,2:T(8,128)(2,1)}, bf16[384,48,128]{0,1,2:T(8,128)(2,1)}, u32[]{:S(2)}, u32[]{:S(2)}) collective-permute-start(bf16[384,48,128]{0,1,2:T(8,128)(2,1)} %collective-permute-done.9), channel_id=1, source_target_pairs={{0,1},{1,2},{2,3},{3,4},{4,5},{5,6},{6,7},{7,8},{8,9},{9,10},{10,1... | collective-permute-start | bytes 14155784 | tf_op jit(solution)/shard_map/ppermute | solution.py:84
  685.8 3.2 collective-permute-start.10
  689.0 8.7 fusion.5
  697.7 92.6 %collective-permute-start.13 = (bf16[384,48,128]{0,1,2:T(8,128)(2,1)}, bf16[384,48,128]{0,1,2:T(8,128)(2,1)}, u32[]{:S(2)}, u32[]{:S(2)}) collective-permute-start(bf16[384,48,128]{0,1,2:T(8,128)(2,1)} %collective-permute-done.11), channel_id=1, source_target_pairs={{0,1},{1,2},{2,3},{3,4},{4,5},{5,6},{6,7},{7,8},{8,9},{9,10},{10,1... | collective-permute-start | bytes 14155784 | tf_op jit(solution)/shard_map/ppermute | solution.py:84
  790.3 10.1 copy.115
  800.4 7.3 constant_dynamic-slice_fusion
  846.6 8.4 fusion.20
  855.0 7.9 fusion.29
  862.9 7.9 fusion.30
  870.8 5.5 fusion.27
  876.4 5.5 fusion.28
  881.8 5.3 fusion.25
  887.2 7.7 fusion.26
  894.9 2.8 collective-permute-start.14
  897.8 7.8 fusion.23
  905.5 7.9 fusion.24
  913.5 7.9 fusion.21
  921.4 7.8 fusion.22
  929.2 7.8 fusion.31
  937.0 7.8 fusion.32
  944.8 7.7 fusion.34
  952.4 5.6 fusion.33
  958.0 8.5 collective-permute-done.14
  966.5 49.2 %bitcast_reduce_fusion = (f32[384,48]{0,1:T(8,128)S(1)}, f32[128,48,384]{2,1,0:T(8,128)}) fusion(bf16[48,48,128]{1,0,2:T(8,128)(2,1)S(1)} %copy.151, bf16[384,48,128]{0,1,2:T(8,128)(2,1)} %collective-permute-done.14, f32[128,48,384]{2,1,0:T(8,128)} %fusion.34, f32[128,48,384]{2,1,0:T(8,128)} %fusion.33, f32[128,48,384]{2,1,0:T(8,128)} %fusion.32, ...), kind=kOutput, calls=%fused_computation.30 | convolution fusion | flops 264222720 | bytes 156377088 | tf_op jit(solution)/shard_map/ikc,jkc->ijc/dot_general | solution.py:95
  1015.8 4.8 multiply_reduce_fusion
  1022.1 3.8 add_convert_fusion
  1026.0 7.6 copy.135
  1033.5 8.6 fusion.4
  1042.2 166.7 %all-gather.5.cloned.1.call-done = bf16[384,192,128]{2,1,0:T(8,128)(2,1)} async-done(((bf16[384,48,128]{2,1,0:T(8,128)(2,1)}), bf16[384,192,128]{2,1,0:T(8,128)(2,1)}) %all-gather.5.cloned.1.call-update) | async-done | bytes 18874384 | tf_op jit(solution)/shard_map/all_gather | solution.py:104
  1208.9 17.8 %copy.153 = bf16[384,192,128]{2,1,0:T(8,128)(2,1)} copy(bf16[384,192,128]{2,1,0:T(8,128)(2,1)} %all-gather.5.cloned.1.call-done) | data formatting | bytes 37748736
  (117 shorter events, 43.8 us)
Async XLA Ops:
  6.5 19.7 %copy-start = (bf16[128,512]{1,0:T(8,128)(2,1)S(1)}, bf16[128,512]{1,0:T(8,128)(2,1)}, u32[]{:S(2)}) copy-start(bf16[128,512]{1,0:T(8,128)(2,1)} %param.14) | copy-start | bytes 393220
  6.5 268.6 %all-gather.3.cloned.1.call-start = ((), (), s32[]{:S(2)}) async-start(), calls=%async_computation.1 | async-start | bytes 14155776 | tf_op jit(solution)/shard_map/all_gather | solution.py:66
  6.5 12.6 %copy-start.25 = (f32[128]{0:T(128)S(1)}, f32[128]{0:T(128)}, u32[]{:S(2)}) copy-start(f32[128]{0:T(128)} %param.13) | copy-start | bytes 1540
  6.5 12.6 %copy-start.26 = (f32[128]{0:T(128)S(1)}, f32[128]{0:T(128)}, u32[]{:S(2)}) copy-start(f32[128]{0:T(128)} %param.12) | copy-start | bytes 1540
  19.2 7.1 copy-start.21
  26.2 14.8 %copy-start.3 = (bf16[384,48,128]{2,1,0:T(8,128)(2,1)}, bf16[384,48,128]{2,1,0:T(8,128)(2,1)S(1)}, u32[]{:S(2)}) copy-start(bf16[384,48,128]{2,1,0:T(8,128)(2,1)S(1)} %fusion.11) | copy-start | bytes 14155780
  66.4 57.7 %collective-permute-start.1 = (bf16[384,48,128]{0,1,2:T(8,128)(2,1)}, bf16[384,48,128]{0,1,2:T(8,128)(2,1)}, u32[]{:S(2)}, u32[]{:S(2)}) collective-permute-start(bf16[384,48,128]{0,1,2:T(8,128)(2,1)} %copy.117), channel_id=1, source_target_pairs={{0,1},{1,2},{2,3},{3,4},{4,5},{5,6},{6,7},{7,8},{8,9},{9,10},{10,1... | collective-permute-start | bytes 14155784 | tf_op jit(solution)/shard_map/ppermute | solution.py:84
  66.9 622.1 %copy-start.27 = (bf16[128,128]{1,0:T(8,128)(2,1)S(1)}, bf16[128,128]{1,0:T(8,128)(2,1)}, u32[]{:S(2)}) copy-start(bf16[128,128]{1,0:T(8,128)(2,1)} %param.16) | copy-start | bytes 98308
  66.9 622.1 %copy-start.28 = (f32[128]{0:T(128)S(1)}, f32[128]{0:T(128)}, u32[]{:S(2)}) copy-start(f32[128]{0:T(128)} %param.17) | copy-start | bytes 1540
  66.9 104.5 %collective-permute-start = (bf16[384,48,128]{0,1,2:T(8,128)(2,1)}, bf16[384,48,128]{0,1,2:T(8,128)(2,1)}, u32[]{:S(2)}, u32[]{:S(2)}) collective-permute-start(bf16[384,48,128]{0,1,2:T(8,128)(2,1)} %copy.117), channel_id=1, source_target_pairs={{0,15},{1,0},{2,1},{3,2},{4,3},{5,4},{6,5},{7,6},{8,7},{9,8},{10,9... | collective-permute-start | bytes 14155784 | tf_op jit(solution)/shard_map/ppermute | solution.py:86
  124.1 56.7 %collective-permute-start.3 = (bf16[384,48,128]{0,1,2:T(8,128)(2,1)}, bf16[384,48,128]{0,1,2:T(8,128)(2,1)}, u32[]{:S(2)}, u32[]{:S(2)}) collective-permute-start(bf16[384,48,128]{0,1,2:T(8,128)(2,1)} %collective-permute-done.1), channel_id=1, source_target_pairs={{0,1},{1,2},{2,3},{3,4},{4,5},{5,6},{6,7},{7,8},{8,9},{9,10},{10,1... | collective-permute-start | bytes 14155784 | tf_op jit(solution)/shard_map/ppermute | solution.py:84
  171.4 109.8 %collective-permute-start.2 = (bf16[384,48,128]{0,1,2:T(8,128)(2,1)}, bf16[384,48,128]{0,1,2:T(8,128)(2,1)}, u32[]{:S(2)}, u32[]{:S(2)}) collective-permute-start(bf16[384,48,128]{0,1,2:T(8,128)(2,1)} %collective-permute-done), channel_id=1, source_target_pairs={{0,15},{1,0},{2,1},{3,2},{4,3},{5,4},{6,5},{7,6},{8,7},{9,8},{10,9... | collective-permute-start | bytes 14155784 | tf_op jit(solution)/shard_map/ppermute | solution.py:86
  180.7 104.9 %collective-permute-start.5 = (bf16[384,48,128]{0,1,2:T(8,128)(2,1)}, bf16[384,48,128]{0,1,2:T(8,128)(2,1)}, u32[]{:S(2)}, u32[]{:S(2)}) collective-permute-start(bf16[384,48,128]{0,1,2:T(8,128)(2,1)} %collective-permute-done.3), channel_id=1, source_target_pairs={{0,1},{1,2},{2,3},{3,4},{4,5},{5,6},{6,7},{7,8},{8,9},{9,10},{10,1... | collective-permute-start | bytes 14155784 | tf_op jit(solution)/shard_map/ppermute | solution.py:84
  275.1 515.2 %all-to-all-start = ((bf16[768,48,128]{2,1,0:T(8,128)(2,1)}), bf16[768,48,128]{2,1,0:T(8,128)(2,1)}, u32[]{:S(2)}, u32[]{:S(2)}) async-start(bf16[768,48,128]{2,1,0:T(8,128)(2,1)} %all-gather.3.cloned.1.call-done), calls=%async_computation | async-start | bytes 18874368 | tf_op jit(solution)/shard_map/all_to_all | solution.py:67
  281.2 927.7 %all-gather.5.cloned.1.call-start = ((), (), s32[]{:S(2)}) async-start(), calls=%async_computation.2 | async-start | bytes 23592960 | tf_op jit(solution)/shard_map/all_gather | solution.py:104
  281.3 203.8 %collective-permute-start.4 = (bf16[384,48,128]{0,1,2:T(8,128)(2,1)}, bf16[384,48,128]{0,1,2:T(8,128)(2,1)S(1)}, u32[]{:S(2)}, u32[]{:S(2)}) collective-permute-start(bf16[384,48,128]{0,1,2:T(8,128)(2,1)} %collective-permute-done.2), channel_id=1, source_target_pairs={{0,15},{1,0},{2,1},{3,2},{4,3},{5,4},{6,5},{7,6},{8,7},{9,8},{10,9... | collective-permute-start | bytes 14155784 | tf_op jit(solution)/shard_map/ppermute | solution.py:86
  285.6 206.2 %collective-permute-start.7 = (bf16[384,48,128]{0,1,2:T(8,128)(2,1)}, bf16[384,48,128]{0,1,2:T(8,128)(2,1)S(1)}, u32[]{:S(2)}, u32[]{:S(2)}) collective-permute-start(bf16[384,48,128]{0,1,2:T(8,128)(2,1)} %collective-permute-done.5), channel_id=1, source_target_pairs={{0,1},{1,2},{2,3},{3,4},{4,5},{5,6},{6,7},{7,8},{8,9},{9,10},{10,1... | collective-permute-start | bytes 14155784 | tf_op jit(solution)/shard_map/ppermute | solution.py:84
  487.2 145.1 %collective-permute-start.6 = (bf16[384,48,128]{0,1,2:T(8,128)(2,1)S(1)}, bf16[384,48,128]{0,1,2:T(8,128)(2,1)S(1)}, u32[]{:S(2)}, u32[]{:S(2)}) collective-permute-start(bf16[384,48,128]{0,1,2:T(8,128)(2,1)S(1)} %collective-permute-done.4), channel_id=1, source_target_pairs={{0,15},{1,0},{2,1},{3,2},{4,3},{5,4},{6,5},{7,6},{8,7},{9,8},{10,9... | collective-permute-start | bytes 14155784 | tf_op jit(solution)/shard_map/ppermute | solution.py:86
  491.9 140.5 %copy-start.18 = (bf16[384,48,128]{0,1,2:T(8,128)(2,1)}, bf16[384,48,128]{0,1,2:T(8,128)(2,1)S(1)}, u32[]{:S(2)}) copy-start(bf16[384,48,128]{0,1,2:T(8,128)(2,1)S(1)} %collective-permute-done.7) | copy-start | bytes 14155780
  491.9 148.1 %collective-permute-start.9 = (bf16[384,48,128]{0,1,2:T(8,128)(2,1)S(1)}, bf16[384,48,128]{0,1,2:T(8,128)(2,1)}, u32[]{:S(2)}, u32[]{:S(2)}) collective-permute-start(bf16[384,48,128]{0,1,2:T(8,128)(2,1)S(1)} %collective-permute-done.7), channel_id=1, source_target_pairs={{0,1},{1,2},{2,3},{3,4},{4,5},{5,6},{6,7},{7,8},{8,9},{9,10},{10,1... | collective-permute-start | bytes 14155784 | tf_op jit(solution)/shard_map/ppermute | solution.py:84
  632.3 7.7 copy-start.19
  632.3 53.4 %collective-permute-start.8 = (bf16[384,48,128]{0,1,2:T(8,128)(2,1)S(1)}, bf16[384,48,128]{0,1,2:T(8,128)(2,1)}, u32[]{:S(2)}, u32[]{:S(2)}) collective-permute-start(bf16[384,48,128]{0,1,2:T(8,128)(2,1)S(1)} %collective-permute-done.6), channel_id=1, source_target_pairs={{0,15},{1,0},{2,1},{3,2},{4,3},{5,4},{6,5},{7,6},{8,7},{9,8},{10,9... | collective-permute-start | bytes 14155784 | tf_op jit(solution)/shard_map/ppermute | solution.py:86
  640.0 57.7 %collective-permute-start.11 = (bf16[384,48,128]{0,1,2:T(8,128)(2,1)}, bf16[384,48,128]{0,1,2:T(8,128)(2,1)}, u32[]{:S(2)}, u32[]{:S(2)}) collective-permute-start(bf16[384,48,128]{0,1,2:T(8,128)(2,1)} %collective-permute-done.9), channel_id=1, source_target_pairs={{0,1},{1,2},{2,3},{3,4},{4,5},{5,6},{6,7},{7,8},{8,9},{9,10},{10,1... | collective-permute-start | bytes 14155784 | tf_op jit(solution)/shard_map/ppermute | solution.py:84
  685.8 201.4 %collective-permute-start.10 = (bf16[384,48,128]{0,1,2:T(8,128)(2,1)}, bf16[384,48,128]{0,1,2:T(8,128)(2,1)}, u32[]{:S(2)}, u32[]{:S(2)}) collective-permute-start(bf16[384,48,128]{0,1,2:T(8,128)(2,1)} %collective-permute-done.8), channel_id=1, source_target_pairs={{0,15},{1,0},{2,1},{3,2},{4,3},{5,4},{6,5},{7,6},{8,7},{9,8},{10,9... | collective-permute-start | bytes 14155784 | tf_op jit(solution)/shard_map/ppermute | solution.py:86
  697.7 197.2 %collective-permute-start.13 = (bf16[384,48,128]{0,1,2:T(8,128)(2,1)}, bf16[384,48,128]{0,1,2:T(8,128)(2,1)}, u32[]{:S(2)}, u32[]{:S(2)}) collective-permute-start(bf16[384,48,128]{0,1,2:T(8,128)(2,1)} %collective-permute-done.11), channel_id=1, source_target_pairs={{0,1},{1,2},{2,3},{3,4},{4,5},{5,6},{6,7},{7,8},{8,9},{9,10},{10,1... | collective-permute-start | bytes 14155784 | tf_op jit(solution)/shard_map/ppermute | solution.py:84
  846.6 8.4 copy-start.16
  855.0 7.9 copy-start.15
  855.0 15.8 %slice-start.4 = ((s8[4718592]{0:T(1024)(128)(4,1)}), s8[4194304]{0:T(1024)(128)(4,1)S(1)}, s32[]{:S(2)}) async-start(s8[4718592]{0:T(1024)(128)(4,1)} %bitcast.65), calls=%async_computation.7 | async-start | bytes 8388608
  862.9 7.9 copy-start.14
  862.9 7.9 slice-start.5
  862.9 13.4 %slice-start.2 = ((s8[4718592]{0:T(1024)(128)(4,1)}), s8[4194304]{0:T(1024)(128)(4,1)S(1)}, s32[]{:S(2)}) async-start(s8[4718592]{0:T(1024)(128)(4,1)} %bitcast.63), calls=%async_computation.5 | async-start | bytes 8388608
  870.8 5.5 copy-start.13
  870.8 11.0 slice-start
  887.2 10.6 copy-start.10
  887.2 65.3 %collective-permute-start.12 = (bf16[384,48,128]{0,1,2:T(8,128)(2,1)}, bf16[384,48,128]{0,1,2:T(8,128)(2,1)S(1)}, u32[]{:S(2)}, u32[]{:S(2)}) collective-permute-start(bf16[384,48,128]{0,1,2:T(8,128)(2,1)} %collective-permute-done.10), channel_id=1, source_target_pairs={{0,15},{1,0},{2,1},{3,2},{4,3},{5,4},{6,5},{7,6},{8,7},{9,8},{10,9... | collective-permute-start | bytes 14155784 | tf_op jit(solution)/shard_map/ppermute | solution.py:86
  894.9 10.6 copy-start.9
  894.9 71.6 %collective-permute-start.14 = (bf16[384,48,128]{0,1,2:T(8,128)(2,1)}, bf16[384,48,128]{0,1,2:T(8,128)(2,1)}, u32[]{:S(2)}, u32[]{:S(2)}) collective-permute-start(bf16[384,48,128]{0,1,2:T(8,128)(2,1)} %collective-permute-done.13), channel_id=1, source_target_pairs={{0,1},{1,2},{2,3},{3,4},{4,5},{5,6},{6,7},{7,8},{8,9},{9,10},{10,1... | collective-permute-start | bytes 14155784 | tf_op jit(solution)/shard_map/ppermute | solution.py:84
  905.5 7.9 copy-start.8
  913.5 7.9 copy-start.7
  921.4 7.8 copy-start.5
  929.2 7.8 copy-start.4
  937.0 7.8 copy-start.6
  1015.8 6.4 copy-start.2
  1015.8 6.4 copy-start.23
  1015.8 6.3 copy-start.24
  1026.0 7.6 copy-start.20
  1026.0 7.6 copy-start.22
  1208.9 17.8 %copy-start.1 = (bf16[128,512]{1,0:T(8,128)(2,1)S(1)}, bf16[128,512]{1,0:T(8,128)(2,1)}, u32[]{:S(2)}) copy-start(bf16[128,512]{1,0:T(8,128)(2,1)} %param.14) | copy-start | bytes 393220
  (5 other events, 23.9 us)
Sparse Core Ops, SparseCore 0:
  67.0 120.5 all-gather.2
  1042.3 166.5 all-gather.4
